TPU v7x, 32 devices: a whole 2x2x4 slice. The times are simulated.
32 devices in a mesh: gx: 2 (over x), gy: 4 (over z), gz: 4 (over y, core).
Axes of the slice: x: 2, y: 2, z: 4, core: 2. Of those that a mesh axis runs over, the one named last changes fastest.
Arguments:
- populations: float32 [39, 16, 96, 512], P(None, 'gx', 'gy', 'gz'), may hold values from 0.5 to 1.5
- relax: float32 [16, 96, 512], P('gx', 'gy', 'gz'), may hold values from 0.6 to 1.9
Outputs:
- advanced: float32 [39, 16, 96, 512], P(None, 'gx', 'gy', 'gz')
All inputs are finite; a program needn't handle non-finite values.
Results may differ from a plain program's by a relative error of at most 0.0001.
Values sent between devices are 32-bit elements; how exact they have to be, the bound alone decides.
No kernel may reach another device: no remote copies, remote signals or barrier semaphores. Data moves between devices by JAX's collectives and lax.ppermute only.
A program may use at most 128 MiB of HBM per device.

v0:
```python
import jax
import jax.numpy as jnp
from jax import lax
from jax.sharding import PartitionSpec as P


def from_behind(block, axis, distance):
    devices = range(lax.axis_size(axis))
    route = [((i - distance) % len(devices), i) for i in devices]
    return lax.ppermute(block, axis, route)


def lattice():
    speeds = [(0, 0, 0)]
    weights = [1.0 / 12.0]
    for axis in range(3):
        for sign in (1, -1):
            vector = [0, 0, 0]
            vector[axis] = sign
            speeds.append(tuple(vector))
            weights.append(1.0 / 12.0)
    for first in (1, -1):
        for second in (1, -1):
            for third in (1, -1):
                speeds.append((first, second, third))
                weights.append(1.0 / 27.0)
    for axis in range(3):
        for sign in (2, -2):
            vector = [0, 0, 0]
            vector[axis] = sign
            speeds.append(tuple(vector))
            weights.append(2.0 / 135.0)
    for couple in ((0, 1), (0, 2), (1, 2)):
        for first in (2, -2):
            for second in (2, -2):
                vector = [0, 0, 0]
                vector[couple[0]] = first
                vector[couple[1]] = second
                speeds.append(tuple(vector))
                weights.append(1.0 / 432.0)
    for axis in range(3):
        for sign in (3, -3):
            vector = [0, 0, 0]
            vector[axis] = sign
            speeds.append(tuple(vector))
            weights.append(1.0 / 1620.0)
    return (speeds, weights)


def collide(popul, rate):
    speeds, weights = lattice()
    acoustic_wave_rate = 2.0 / 3.0
    inverse = 1.0 / acoustic_wave_rate**0.5
    zeroth_moment_rho = sum((weights[member] * popul[member] for member in range(39)))
    flux = [
        sum(
            (
                weights[member] * speeds[member][axis] * popul[member]
                for member in range(39)
                if speeds[member][axis] != 0
            )
        )
        for axis in range(3)
    ]
    thermal_heat_content = sum(
        (
            weights[member]
            * float(sum((value * value for value in speeds[member])))
            * popul[member]
            for member in range(1, 39)
        )
    )
    velocity = [part / zeroth_moment_rho for part in flux]
    flow_norm_square = (
        velocity[0] * velocity[0] + velocity[1] * velocity[1] + velocity[2] * velocity[2]
    )
    site_kinetic_heat = (thermal_heat_content / zeroth_moment_rho - flow_norm_square) / (
        3.0 * acoustic_wave_rate
    )
    scaled = [part * inverse for part in velocity]
    scaled_square = flow_norm_square / acoustic_wave_rate
    excess_quantity = site_kinetic_heat - 1.0
    results = []
    for member in range(39):
        vector = speeds[member]
        aligned = (
            sum((vector[axis] * inverse * scaled[axis] for axis in range(3) if vector[axis] != 0))
            if member > 0
            else jnp.zeros_like(zeroth_moment_rho)
        )
        speed_square = float(sum((value * value for value in vector))) / acoustic_wave_rate
        aligned_square = aligned * aligned
        hermite = (
            1.0
            + aligned
            + 0.5 * (aligned_square - scaled_square + excess_quantity * (speed_square - 3.0))
            + aligned
            * (aligned_square - 3.0 * scaled_square + 3.0 * excess_quantity * (speed_square - 5.0))
            / 6.0
            + (
                aligned_square * aligned_square
                - 6.0 * aligned_square * scaled_square
                + 3.0 * scaled_square * scaled_square
                + 6.0
                * excess_quantity
                * (aligned_square * (speed_square - 7.0) + scaled_square * (5.0 - speed_square))
                + 3.0
                * excess_quantity
                * excess_quantity
                * (speed_square * speed_square - 10.0 * speed_square + 15.0)
            )
            / 24.0
        )
        maxwellian_target = zeroth_moment_rho * hermite
        results.append(popul[member] - rate * (popul[member] - maxwellian_target))
    return jnp.stack(results)


def propagate(extended, depth):
    speeds, weights = lattice()
    lengths = [extended.shape[dim] - 2 * depth for dim in (1, 2, 3)]
    results = []
    for member in range(39):
        vector = speeds[member]
        starts = [depth - vector[axis] for axis in range(3)]
        results.append(
            extended[
                member,
                starts[0] : starts[0] + lengths[0],
                starts[1] : starts[1] + lengths[1],
                starts[2] : starts[2] + lengths[2],
            ]
        )
    return jnp.stack(results)


def outbound(full, dim, sign):
    speeds, weights = lattice()
    count = full.shape[dim]
    slabs = []
    for member in range(39):
        speed = speeds[member][dim - 1] * sign
        if speed > 0:
            field = full[member]
            if sign > 0:
                layers = lax.slice_in_dim(field, count - speed, count, axis=dim - 1)
            else:
                layers = lax.slice_in_dim(field, 0, speed, axis=dim - 1)
            slabs.append(jnp.moveaxis(layers, dim - 1, 0))
    return jnp.concatenate(slabs, axis=0)


def empty_layers(field, axis, count):
    shape = list(field.shape)
    shape[axis] = count
    return jnp.zeros(tuple(shape), jnp.float32)


def inbound(full, dim, from_lower, from_upper):
    speeds, weights = lattice()
    axis = dim - 1
    lower_offset = 0
    upper_offset = 0
    layers = []
    for member in range(39):
        field = full[member]
        speed = speeds[member][axis]
        if speed > 0:
            slab = jnp.moveaxis(from_lower[lower_offset : lower_offset + speed], 0, axis)
            lower_offset = lower_offset + speed
            below = jnp.concatenate([empty_layers(field, axis, 3 - speed), slab], axis=axis)
            above = empty_layers(field, axis, 3)
        elif speed < 0:
            slab = jnp.moveaxis(from_upper[upper_offset : upper_offset - speed], 0, axis)
            upper_offset = upper_offset - speed
            below = empty_layers(field, axis, 3)
            above = jnp.concatenate([slab, empty_layers(field, axis, 3 + speed)], axis=axis)
        else:
            below = empty_layers(field, axis, 3)
            above = empty_layers(field, axis, 3)
        layers.append(jnp.concatenate([below, field, above], axis=axis))
    return jnp.stack(layers)


def per_device(populations, relax):
    state = populations
    post = collide(state, relax)
    from_lower = from_behind(outbound(post, 1, 1), "gx", 1)
    from_upper = from_behind(outbound(post, 1, -1), "gx", -1)
    extended = inbound(post, 1, from_lower, from_upper)
    from_lower = from_behind(outbound(extended, 2, 1), "gy", 1)
    from_upper = from_behind(outbound(extended, 2, -1), "gy", -1)
    extended = inbound(extended, 2, from_lower, from_upper)
    from_lower = from_behind(outbound(extended, 3, 1), "gz", 1)
    from_upper = from_behind(outbound(extended, 3, -1), "gz", -1)
    extended = inbound(extended, 3, from_lower, from_upper)
    state = propagate(extended, 3)
    return state


def solution(mesh):
    return jax.shard_map(
        per_device,
        mesh=mesh,
        in_specs=(P(None, "gx", "gy", "gz"), P("gx", "gy", "gz")),
        out_specs=P(None, "gx", "gy", "gz"),
        check_vma=False,
    )
```

profile of v0, /device:TPU:0, one launch (start us, length us, event | category | flops | bytes accessed | tf_op | source)
XLA Modules:
  0.0 99.0 jit_solution(3598783697626491069)
XLA Ops:
  0.0 3.4 %bitcast_subtract_fusion = (f32[8,24,128]{2,1,0:T(8,128)S(1)}, f32[8,24,128]{2,1,0:T(8,128)S(1)}, f32[8,24,128]{2,1,0:T(8,128)S(1)}, f32[8,24,128]{2,1,0:T(8,128...) fusion(f32[8,24,128]{2,1,0:T(8,128)} %param.3, f32[39,8,24,128]{3,2,1,0:T(8,128)} %param.2), kind=kLoop, calls=%fused_computation.549 | loop fusion | flops 7348224 | bytes 4620288 | tf_op jit(solution)/shard_map/sub | solution.py:115
  3.5 1.2 %bitcast_subtract_fusion.4 = (f32[8,24,128]{2,1,0:T(8,128)S(1)}, f32[8,24,128]{2,1,0:T(8,128)S(1)}, f32[8,24,128]{2,1,0:T(8,128)S(1)}, f32[8,24,128]{2,1,0:T(8,1...) fusion(f32[8,24,128]{2,1,0:T(8,128)S(1)} %copy-done.1, ...), kind=kLoop, calls=%fused_computation.572 | loop fusion | flops 9363456 | bytes 3145728 | tf_op jit(solution)/shard_map/sub | solution.py:115
  4.8 1.2 %bitcast_subtract_fusion.12 = (f32[8,24,128]{2,1,0:T(8,128)S(1)}, f32[8,24,128]{2,1,0:T(8,128)S(1)}, f32[8,24,128]{2,1,0:T(8,128)S(1)}, f32[8,24,128]{2,1,0:T(8,...) fusion(f32[8,24,128]{2,1,0:T(8,128)S(1)} %copy-done.1, ...), kind=kLoop, calls=%fused_computation.610 | loop fusion | flops 8945664 | bytes 3047424 | tf_op jit(solution)/shard_map/sub | solution.py:115
  5.9 1.2 %bitcast_subtract_fusion.36 = (f32[8,24,128]{2,1,0:T(8,128)S(1)}, f32[8,24,128]{2,1,0:T(8,128)S(1)}, f32[8,24,128]{2,1,0:T(8,128)S(1)}, f32[8,24,128]{2,1,0:T(8,...) fusion(f32[8,24,128]{2,1,0:T(8,128)S(1)} %copy-done.1, ...), kind=kLoop, calls=%fused_computation.733 | loop fusion | flops 9461760 | bytes 3145728 | tf_op jit(solution)/shard_map/sub | solution.py:115
  7.5 3.0 %collective-permute-start.1 = (f32[18,24,128]{2,1,0:T(8,128)S(1)}, f32[18,24,128]{2,1,0:T(8,128)S(1)}, u32[]{:S(2)}, u32[]{:S(2)}) collective-permute-start(f32[18,24,128]{2,1,0:T(8,128)S(1)} %constant_dynamic-update-slice_fusion.11), channel_id=1, source_target_pairs={{16,0},{0,16},{17,1},{1,17},{18,2},{2,18},{19,3},{3,19},{20,4},{4,... | collective-permute-start | bytes 663560 | tf_op jit(solution)/shard_map/ppermute | solution.py:10
  14.1 2.7 %collective-permute-done.1 = f32[18,24,128]{2,1,0:T(8,128)S(1)} collective-permute-done((f32[18,24,128]{2,1,0:T(8,128)S(1)}, f32[18,24,128]{2,1,0:T(8,128)S(1)}, u32[]{:S(2)}, u32[]{:S(2)}) %collective-permute-start.1) | collective-permute-done | bytes 221216 | tf_op jit(solution)/shard_map/ppermute | solution.py:10
  17.4 3.2 %collective-permute-done = f32[18,24,128]{2,1,0:T(8,128)S(1)} collective-permute-done((f32[18,24,128]{2,1,0:T(8,128)S(1)}, f32[18,24,128]{2,1,0:T(8,128)S(1)}, u32[]{:S(2)}, u32[]{:S(2)}) %collective-permute-start) | collective-permute-done | bytes 221216 | tf_op jit(solution)/shard_map/ppermute | solution.py:10
  23.8 3.9 %collective-permute-start.3 = (f32[18,14,128]{2,0,1:T(8,128)S(1)}, f32[18,14,128]{2,0,1:T(8,128)}, u32[]{:S(2)}, u32[]{:S(2)}) collective-permute-start(f32[18,14,128]{2,0,1:T(8,128)S(1)} %concatenate.405), channel_id=1, source_target_pairs={{4,0},{8,4},{12,8},{0,12},{5,1},{9,5},{13,9},{1,13},{6,2},{10,6},{... | collective-permute-start | bytes 387080 | tf_op jit(solution)/shard_map/ppermute | solution.py:10
  27.7 2.6 %concatenate.391 = f32[18,14,128]{2,0,1:T(8,128)S(1)} concatenate(f32[1,14,128]{2,0,1:T(1,128)} %get-tuple-element.206, f32[1,14,128]{2,0,1:T(1,128)} %get-tuple-element.191, f32[1,14,128]{2,0,1:T(1,128)} %get-tuple-element.186, f32[1,14,128]{2,0,1:T(1,128)} %get-tuple-element.190, f32[1,14,128]{2,0,1:T(1,128)} %get-tuple-element.187, f32[2,14,128]{2,0,1:T(2,128)S(1)} %get-tuple-element.203, ...), dimensions={0} | concatenate | bytes 258048 | tf_op jit(solution)/shard_map/concatenate | solution.py:150
  30.4 1.4 %fusion.87 = (f32[1,14,30,134]{3,2,1,0:T(8,128)}, f32[1,14,30,134]{3,2,1,0:T(8,128)}) fusion(f32[14,30,3]{2,1,0:T(8,128)S(1)} %broadcast.262, f32[14,3,128]{2,1,0:T(4,128)S(1)} %broadcast.263, f32[1,24,128]{2,1,0:T(8,128)S(1)} %broadcast.303, f32[3,24,128]{2,1,0:T(8,128)S(1)} %broadcast.264, f32[2,24,128]{2,1,0:T(8,128)S(1)} %get-tuple-element.124, ...), kind=kLoop, calls=%fused_computation.347 | loop fusion | flops 787920 | bytes 771696 | tf_op jit(solution)/shard_map/stack | solution.py:182
  31.7 1.0 %fusion.148 = (f32[2,14,30]{0,2,1:T(8,128)}, f32[2,14,30]{0,2,1:T(8,128)}, f32[2,14,30]{0,2,1:T(8,128)}) fusion(f32[14,3,128]{2,1,0:T(4,128)S(1)} %broadcast.263, f32[3,24,128]{2,1,0:T(8,128)S(1)} %broadcast.264, f32[1,24,128]{2,1,0:T(8,128)S(1)} %broadcast.303, f32[2,24,128]{2,1,0:T(8,128)S(1)} %get-tuple-element.125, ...), kind=kLoop, calls=%fused_computation.448 | loop fusion | flops 12600 | bytes 449376 | tf_op jit(solution)/shard_map/transpose | solution.py:149
  32.7 1.8 %slice_bitcast_fusion.34 = (f32[14,1,128]{2,1,0:T(1,128)S(1)}, f32[14,1,128]{2,1,0:T(1,128)S(1)}, f32[14,1,128]{2,1,0:T(1,128)S(1)}, f32[14,1,128]{2,1,0:T(1,128)}, f32[14,1,128]{2,1,0:T(1,128)}) fusion(f32[18,14,128]{2,0,1:T(8,128)} %collective-permute-done.3), kind=kLoop, calls=%fused_computation.1191 | loop fusion | bytes 71680 | tf_op jit(solution)/shard_map/transpose | solution.py:174
  35.5 2.0 %collective-permute-done.2 = f32[18,14,128]{2,0,1:T(8,128)S(1)} collective-permute-done((f32[18,14,128]{2,0,1:T(8,128)S(1)}, f32[18,14,128]{2,0,1:T(8,128)S(1)}, u32[]{:S(2)}, u32[]{:S(2)}) %collective-permute-start.2) | collective-permute-done | bytes 129056 | tf_op jit(solution)/shard_map/ppermute | solution.py:10
  38.2 1.1 %fusion.115 = (f32[1,14,30]{0,2,1:T(8,128)}, f32[1,14,30]{0,2,1:T(8,128)}, f32[1,14,30]{0,2,1:T(8,128)}) fusion(f32[14,2,128]{2,1,0:T(2,128)S(1)} %broadcast.302, f32[2,24,128]{2,1,0:T(8,128)S(1)} %broadcast.288, f32[3,24,128]{2,1,0:T(8,128)S(1)} %broadcast.264, f32[14,3,128]{2,1,0:T(4,128)S(1)} %broadcast.263, f32[14,1,128]{2,1,0:T(1,128)S(1)} %get-tuple-element.154, ...), kind=kLoop, calls=%fused_computation.415 | loop fusion | flops 6720 | bytes 436144 | tf_op jit(solution)/shard_map/transpose | solution.py:149
  39.3 1.0 %fusion.129 = (f32[1,14,30]{0,2,1:T(8,128)}, f32[1,14,30]{0,2,1:T(8,128)}, f32[1,14,30]{0,2,1:T(8,128)}) fusion(f32[14,3,128]{2,1,0:T(4,128)S(1)} %broadcast.263, f32[2,24,128]{2,1,0:T(8,128)S(1)} %broadcast.288, f32[3,24,128]{2,1,0:T(8,128)S(1)} %broadcast.264, f32[14,2,128]{2,1,0:T(2,128)S(1)} %broadcast.302, f32[14,1,128]{2,1,0:T(1,128)S(1)} %get-tuple-element.159, ...), kind=kLoop, calls=%fused_computation.429 | loop fusion | flops 6720 | bytes 436144 | tf_op jit(solution)/shard_map/transpose | solution.py:149
  41.3 1.7 %slice_bitcast_fusion.24 = (f32[14,2,128]{2,1,0:T(2,128)}, f32[14,2,128]{2,1,0:T(2,128)}, f32[14,2,128]{2,1,0:T(2,128)}, f32[14,2,128]{2,1,0:T(2,128)S(1)}, f32[14,2,128]{2,1,0:T(2,128)S(1)}) fusion(f32[18,14,128]{2,0,1:T(8,128)} %collective-permute-done.3), kind=kLoop, calls=%fused_computation.1139 | loop fusion | bytes 143360 | tf_op jit(solution)/shard_map/transpose | solution.py:174
  43.9 2.7 %concatenate.442 = f32[18,14,30]{0,2,1:T(8,128)} concatenate(f32[1,14,30]{0,2,1:T(8,128)} %get-tuple-element.183, f32[1,14,30]{0,2,1:T(8,128)} %get-tuple-element.167, f32[1,14,30]{0,2,1:T(8,128)} %get-tuple-element.168, f32[1,14,30]{0,2,1:T(8,128)} %get-tuple-element.166, f32[1,14,30]{0,2,1:T(8,128)} %get-tuple-element.164, f32[2,14,30]{0,2,1:T(8,128)S(1)} %get-tuple-element.180, ...), dimensions={0} | concatenate | bytes 60480 | tf_op jit(solution)/shard_map/concatenate | solution.py:150
  46.6 1.7 %fusion.108 = (f32[1,14,30]{0,2,1:T(8,128)S(1)}, f32[1,14,30]{0,2,1:T(8,128)}) fusion(f32[14,2,128]{2,1,0:T(2,128)S(1)} %broadcast.302, f32[3,24,128]{2,1,0:T(8,128)S(1)} %broadcast.264, f32[2,24,128]{2,1,0:T(8,128)S(1)} %broadcast.288, f32[14,3,128]{2,1,0:T(4,128)S(1)} %broadcast.263, f32[14,1,128]{2,1,0:T(1,128)} %get-tuple-element.157, ...), kind=kLoop, calls=%fused_computation.408 | loop fusion | flops 5040 | bytes 336160 | tf_op jit(solution)/shard_map/transpose | solution.py:149
  48.4 2.6 %concatenate.424 = f32[18,14,30]{0,2,1:T(8,128)} concatenate(f32[1,14,30]{0,2,1:T(8,128)} %get-tuple-element.184, f32[1,14,30]{0,2,1:T(8,128)} %get-tuple-element.171, f32[1,14,30]{0,2,1:T(8,128)S(1)} %get-tuple-element.170, f32[1,14,30]{0,2,1:T(8,128)} %get-tuple-element.165, f32[1,14,30]{0,2,1:T(8,128)} %get-tuple-element.169, f32[2,14,30]{0,2,1:T(8,128)} %fusion.136, ...), dimensions={0} | concatenate | bytes 60480 | tf_op jit(solution)/shard_map/concatenate | solution.py:150
  51.7 1.5 %fusion.89 = (f32[1,14,30,134]{3,2,1,0:T(8,128)S(1)}, f32[1,14,30,134]{3,2,1,0:T(8,128)S(1)}) fusion(f32[14,30,3]{2,1,0:T(8,128)S(1)} %broadcast.262, f32[14,1,128]{2,1,0:T(1,128)S(1)} %broadcast.305, f32[3,24,128]{2,1,0:T(8,128)S(1)} %broadcast.264, f32[14,3,128]{2,1,0:T(4,128)S(1)} %broadcast.263, f32[14,2,128]{2,1,0:T(2,128)} %get-tuple-element.146, ...), kind=kLoop, calls=%fused_computation.349 | loop fusion | flops 787920 | bytes 746096 | tf_op jit(solution)/shard_map/stack | solution.py:182
  53.2 1.4 %fusion.94 = (f32[1,14,30,134]{3,2,1,0:T(8,128)S(1)}, f32[1,14,30,134]{3,2,1,0:T(8,128)S(1)}) fusion(f32[14,30,3]{2,1,0:T(8,128)S(1)} %broadcast.262, f32[14,1,128]{2,1,0:T(1,128)S(1)} %broadcast.305, f32[1,24,128]{2,1,0:T(8,128)S(1)} %broadcast.303, f32[3,24,128]{2,1,0:T(8,128)S(1)} %broadcast.264, f32[14,3,128]{2,1,0:T(4,128)S(1)} %broadcast.263, ...), kind=kLoop, calls=%fused_computation.354 | loop fusion | flops 900480 | bytes 807536 | tf_op jit(solution)/shard_map/stack | solution.py:182
  54.6 1.4 %fusion.93 = (f32[1,14,30,134]{3,2,1,0:T(8,128)S(1)}, f32[1,14,30,134]{3,2,1,0:T(8,128)S(1)}) fusion(f32[14,30,3]{2,1,0:T(8,128)S(1)} %broadcast.262, f32[14,3,128]{2,1,0:T(4,128)S(1)} %broadcast.263, f32[1,24,128]{2,1,0:T(8,128)S(1)} %broadcast.303, f32[3,24,128]{2,1,0:T(8,128)S(1)} %broadcast.264, f32[14,1,128]{2,1,0:T(1,128)S(1)} %broadcast.305, ...), kind=kLoop, calls=%fused_computation.353 | loop fusion | flops 900480 | bytes 807536 | tf_op jit(solution)/shard_map/stack | solution.py:182
  75.4 1.7 %constant_dynamic-update-slice_fusion.45 = f32[39,8,24,128]{3,2,1,0:T(8,128)} fusion(f32[39,8,24,128]{3,2,1,0:T(8,128)} %constant_dynamic-update-slice_fusion.46, f32[1,14,30,134]{3,2,1,0:T(8,128)} %get-tuple-element.93), kind=kLoop, calls=%fused_computation.533 | loop fusion | bytes 196608
  77.1 1.7 %constant_dynamic-update-slice_fusion.44 = f32[39,8,24,128]{3,2,1,0:T(8,128)} fusion(f32[39,8,24,128]{3,2,1,0:T(8,128)} %constant_dynamic-update-slice_fusion.45, f32[1,14,30,134]{3,2,1,0:T(8,128)} %get-tuple-element.92), kind=kLoop, calls=%fused_computation.532 | loop fusion | bytes 196608
  (283 shorter events, 50.7 us)
Async XLA Ops:
  4.7 16.6 %copy-start.14 = (f32[8,24,128]{2,1,0:T(8,128)}, f32[8,24,128]{2,1,0:T(8,128)S(1)}, u32[]{:S(2)}) copy-start(f32[8,24,128]{2,1,0:T(8,128)S(1)} %get-tuple-element.55) | copy-start | bytes 294916
  4.7 17.2 %copy-start.18 = (f32[8,24,128]{2,1,0:T(8,128)}, f32[8,24,128]{2,1,0:T(8,128)S(1)}, u32[]{:S(2)}) copy-start(f32[8,24,128]{2,1,0:T(8,128)S(1)} %get-tuple-element.58) | copy-start | bytes 294916
  7.2 15.5 %copy-start.20 = (f32[8,24,128]{2,1,0:T(8,128)}, f32[8,24,128]{2,1,0:T(8,128)S(1)}, u32[]{:S(2)}) copy-start(f32[8,24,128]{2,1,0:T(8,128)S(1)} %get-tuple-element.42) | copy-start | bytes 294916
  7.2 15.5 %copy-start.24 = (f32[8,24,128]{2,1,0:T(8,128)}, f32[8,24,128]{2,1,0:T(8,128)S(1)}, u32[]{:S(2)}) copy-start(f32[8,24,128]{2,1,0:T(8,128)S(1)} %get-tuple-element.49) | copy-start | bytes 294916
  7.2 15.6 %copy-start.26 = (f32[8,24,128]{2,1,0:T(8,128)}, f32[8,24,128]{2,1,0:T(8,128)S(1)}, u32[]{:S(2)}) copy-start(f32[8,24,128]{2,1,0:T(8,128)S(1)} %get-tuple-element.52) | copy-start | bytes 294916
  7.2 16.2 %copy-start.28 = (f32[8,24,128]{2,1,0:T(8,128)}, f32[8,24,128]{2,1,0:T(8,128)S(1)}, u32[]{:S(2)}) copy-start(f32[8,24,128]{2,1,0:T(8,128)S(1)} %get-tuple-element.51) | copy-start | bytes 294916
  7.2 31.0 %copy-start.12 = (f32[8,24,128]{2,1,0:T(8,128)}, f32[8,24,128]{2,1,0:T(8,128)S(1)}, u32[]{:S(2)}) copy-start(f32[8,24,128]{2,1,0:T(8,128)S(1)} %get-tuple-element.41) | copy-start | bytes 294916
  7.2 32.1 %copy-start.16 = (f32[8,24,128]{2,1,0:T(8,128)}, f32[8,24,128]{2,1,0:T(8,128)S(1)}, u32[]{:S(2)}) copy-start(f32[8,24,128]{2,1,0:T(8,128)S(1)} %get-tuple-element.44) | copy-start | bytes 294916
  7.2 33.8 %copy-start.2 = (f32[8,24,128]{2,1,0:T(8,128)}, f32[8,24,128]{2,1,0:T(8,128)S(1)}, u32[]{:S(2)}) copy-start(f32[8,24,128]{2,1,0:T(8,128)S(1)} %get-tuple-element.40) | copy-start | bytes 294916
  7.5 9.3 %collective-permute-start.1 = (f32[18,24,128]{2,1,0:T(8,128)S(1)}, f32[18,24,128]{2,1,0:T(8,128)S(1)}, u32[]{:S(2)}, u32[]{:S(2)}) collective-permute-start(f32[18,24,128]{2,1,0:T(8,128)S(1)} %constant_dynamic-update-slice_fusion.11), channel_id=1, source_target_pairs={{16,0},{0,16},{17,1},{1,17},{18,2},{2,18},{19,3},{3,19},{20,4},{4,... | collective-permute-start | bytes 663560 | tf_op jit(solution)/shard_map/ppermute | solution.py:10
  10.5 10.2 %collective-permute-start = (f32[18,24,128]{2,1,0:T(8,128)S(1)}, f32[18,24,128]{2,1,0:T(8,128)S(1)}, u32[]{:S(2)}, u32[]{:S(2)}) collective-permute-start(f32[18,24,128]{2,1,0:T(8,128)S(1)} %constant_dynamic-update-slice_fusion), channel_id=1, source_target_pairs={{16,0},{0,16},{17,1},{1,17},{18,2},{2,18},{19,3},{3,19},{20,4},{4,... | collective-permute-start | bytes 663560 | tf_op jit(solution)/shard_map/ppermute | solution.py:10
  17.4 21.9 %copy-start.40 = (f32[1,24,128]{2,1,0:T(8,128)}, f32[1,24,128]{2,1,0:T(8,128)S(1)}, u32[]{:S(2)}) copy-start(f32[1,24,128]{2,1,0:T(8,128)S(1)} %get-tuple-element.134) | copy-start | bytes 36868
  17.4 21.9 %copy-start.42 = (f32[1,24,128]{2,1,0:T(8,128)}, f32[1,24,128]{2,1,0:T(8,128)S(1)}, u32[]{:S(2)}) copy-start(f32[1,24,128]{2,1,0:T(8,128)S(1)} %get-tuple-element.137) | copy-start | bytes 36868
  17.4 21.9 %copy-start.48 = (f32[1,24,128]{2,1,0:T(8,128)}, f32[1,24,128]{2,1,0:T(8,128)S(1)}, u32[]{:S(2)}) copy-start(f32[1,24,128]{2,1,0:T(8,128)S(1)} %get-tuple-element.135) | copy-start | bytes 36868
  17.4 21.9 %copy-start.44 = (f32[1,24,128]{2,1,0:T(8,128)}, f32[1,24,128]{2,1,0:T(8,128)S(1)}, u32[]{:S(2)}) copy-start(f32[1,24,128]{2,1,0:T(8,128)S(1)} %get-tuple-element.136) | copy-start | bytes 36868
  21.3 18.0 %copy-start.50 = (f32[1,24,128]{2,1,0:T(8,128)}, f32[1,24,128]{2,1,0:T(8,128)S(1)}, u32[]{:S(2)}) copy-start(f32[1,24,128]{2,1,0:T(8,128)S(1)} %get-tuple-element.139) | copy-start | bytes 36868
  22.6 18.3 %copy-start.36 = (f32[2,24,128]{2,1,0:T(8,128)}, f32[2,24,128]{2,1,0:T(8,128)S(1)}, u32[]{:S(2)}) copy-start(f32[2,24,128]{2,1,0:T(8,128)S(1)} %get-tuple-element.128) | copy-start | bytes 73732
  22.6 18.3 %copy-start.38 = (f32[2,24,128]{2,1,0:T(8,128)}, f32[2,24,128]{2,1,0:T(8,128)S(1)}, u32[]{:S(2)}) copy-start(f32[2,24,128]{2,1,0:T(8,128)S(1)} %get-tuple-element.127) | copy-start | bytes 73732
  22.7 18.3 %copy-start.32 = (f32[2,24,128]{2,1,0:T(8,128)}, f32[2,24,128]{2,1,0:T(8,128)S(1)}, u32[]{:S(2)}) copy-start(f32[2,24,128]{2,1,0:T(8,128)S(1)} %get-tuple-element.131) | copy-start | bytes 73732
  22.7 18.6 %copy-start.37 = (f32[2,24,128]{2,1,0:T(8,128)}, f32[2,24,128]{2,1,0:T(8,128)S(1)}, u32[]{:S(2)}) copy-start(f32[2,24,128]{2,1,0:T(8,128)S(1)} %get-tuple-element.132) | copy-start | bytes 73732
  23.8 8.9 %collective-permute-start.3 = (f32[18,14,128]{2,0,1:T(8,128)S(1)}, f32[18,14,128]{2,0,1:T(8,128)}, u32[]{:S(2)}, u32[]{:S(2)}) collective-permute-start(f32[18,14,128]{2,0,1:T(8,128)S(1)} %concatenate.405), channel_id=1, source_target_pairs={{4,0},{8,4},{12,8},{0,12},{5,1},{9,5},{13,9},{1,13},{6,2},{10,6},{... | collective-permute-start | bytes 387080 | tf_op jit(solution)/shard_map/ppermute | solution.py:10
  30.3 7.3 %collective-permute-start.2 = (f32[18,14,128]{2,0,1:T(8,128)S(1)}, f32[18,14,128]{2,0,1:T(8,128)S(1)}, u32[]{:S(2)}, u32[]{:S(2)}) collective-permute-start(f32[18,14,128]{2,0,1:T(8,128)S(1)} %concatenate.391), channel_id=1, source_target_pairs={{12,0},{0,4},{4,8},{8,12},{13,1},{1,5},{5,9},{9,13},{14,2},{2,6},{... | collective-permute-start | bytes 387080 | tf_op jit(solution)/shard_map/ppermute | solution.py:10
  46.6 12.2 %collective-permute-start.5 = (f32[18,14,30]{0,2,1:T(8,128)}, f32[18,14,30]{0,2,1:T(8,128)S(1)}, u32[]{:S(2)}, u32[]{:S(2)}) collective-permute-start(f32[18,14,30]{0,2,1:T(8,128)} %concatenate.442), channel_id=1, source_target_pairs={{1,0},{2,1},{3,2},{0,3},{5,4},{6,5},{7,6},{4,7},{9,8},{10,9},{11,1... | collective-permute-start | bytes 90728 | tf_op jit(solution)/shard_map/ppermute | solution.py:10
  51.0 9.7 %collective-permute-start.4 = (f32[18,14,30]{0,2,1:T(8,128)}, f32[18,14,30]{0,2,1:T(8,128)S(1)}, u32[]{:S(2)}, u32[]{:S(2)}) collective-permute-start(f32[18,14,30]{0,2,1:T(8,128)} %concatenate.424), channel_id=1, source_target_pairs={{3,0},{0,1},{1,2},{2,3},{7,4},{4,5},{5,6},{6,7},{11,8},{8,9},{9,10... | collective-permute-start | bytes 90728 | tf_op jit(solution)/shard_map/ppermute | solution.py:10
  (66 other events, 348.8 us)
where the time goes:
time: 100 us; the launch traced here: 99 us
  local copies, waits for them, and re-layouts  48.8 us (49%)
  other arithmetic  33.1 us (33%)
  waiting for transfers between devices  7.9 us (8%)
  starting transfers between devices  7.83 us (8%)
  between operations  1.28 us (1%)
    unnamed x221, local copies, waits for them, and re-layouts  30.2 us
    another operation x20, other arithmetic, inbound(): return jnp.stack(layers)  15 us
    transpose x14, other arithmetic, outbound(): slabs.append(jnp.moveaxis(layers, dim - 1, 0))  11.1 us
    concatenate x6, local copies, waits for them, and re-layouts, outbound(): return jnp.concatenate(slabs, axis=0)  8.28 us
    ppermute x6, waiting for transfers between devices, from_behind(): return lax.ppermute(block, axis, route)  7.9 us
    ppermute x6, starting transfers between devices, from_behind(): return lax.ppermute(block, axis, route)  7.83 us
    sub x4, other arithmetic, collide(): results.append(popul[member] - rate * (popul[member] - maxwellian_target))  7.04 us
    transpose x6, local copies, waits for them, and re-layouts, inbound(): slab = jnp.moveaxis(from_upper[upper_offset:upper_offset - speed], 0, axis)  5.21 us
  transfers between devices with their start and end apart: 6, of which 3 were waited for; matrix products, arithmetic and copies ran while one was open for 25% of the time, Pallas kernels for 0%

commit v1 on v0

v1 whole, which is shorter than its diff:
```python
import jax
import jax.numpy as jnp
from jax import lax
from jax.experimental import pallas as pl
from jax.experimental.pallas import tpu as pltpu
from jax.sharding import PartitionSpec as P


def lattice():
    speeds = [(0, 0, 0)]
    weights = [1.0 / 12.0]

    def unit(axis, value):
        return tuple(value if axis == other else 0 for other in range(3))

    for axis in range(3):
        for sign in (1, -1):
            speeds.append(unit(axis, sign))
            weights.append(1.0 / 12.0)
    for first in (1, -1):
        for second in (1, -1):
            for third in (1, -1):
                speeds.append((first, second, third))
                weights.append(1.0 / 27.0)
    for axis in range(3):
        for sign in (2, -2):
            speeds.append(unit(axis, sign))
            weights.append(2.0 / 135.0)
    for couple in ((0, 1), (0, 2), (1, 2)):
        for first in (2, -2):
            for second in (2, -2):
                vector = [0, 0, 0]
                vector[couple[0]] = first
                vector[couple[1]] = second
                speeds.append(tuple(vector))
                weights.append(1.0 / 432.0)
    for axis in range(3):
        for sign in (3, -3):
            speeds.append(unit(axis, sign))
            weights.append(1.0 / 1620.0)
    return speeds, weights


SPEEDS, WEIGHTS = lattice()
Q = len(SPEEDS)
OPPOSITE = [SPEEDS.index(tuple(-v for v in c)) for c in SPEEDS]
PAIRS = [(m, OPPOSITE[m]) for m in range(Q) if m < OPPOSITE[m]]
F32 = jnp.float32

ZOFF = {}
_next = 0
for _sign in (1, -1):
    for _m in range(Q):
        if SPEEDS[_m][2] * _sign > 0:
            ZOFF[_m] = _next
            _next += abs(SPEEDS[_m][2])
ZHALF = _next // 2

XOFF = {}
_next = 0
for _sign in (1, -1):
    for _m in range(Q):
        if SPEEDS[_m][0] * _sign > 0:
            XOFF[_m] = _next
            _next += abs(SPEEDS[_m][0])
XHALF = _next // 2

YOFF = {}
for _sign in (1, -1):
    _next = 0
    for _m in range(Q):
        if SPEEDS[_m][1] * _sign > 0:
            YOFF[_m] = _next
            _next += abs(SPEEDS[_m][1])
YCOUNT = _next

EOFF = {}
_next = 0
for _sign in (1, -1):
    for _m in range(Q):
        if SPEEDS[_m][0] * _sign > 0 and SPEEDS[_m][1] != 0:
            EOFF[_m] = _next
            _next += abs(SPEEDS[_m][0]) * abs(SPEEDS[_m][1])
ECOUNT = _next


def wrapped_rows(speed, count):
    return range(speed) if speed > 0 else range(count + speed, count)


def z_home(member, lanes):
    speed = SPEEDS[member][2]
    lane = lax.broadcasted_iota(jnp.int32, (1, lanes), 1)
    if speed > 0:
        return (-ZOFF[member]) % lanes, lane < speed
    return (lanes + speed - ZOFF[member]) % lanes, lane >= lanes + speed


def collide_rows(load, rate, store):
    total = load(0)
    groups = {}
    flux = [None, None, None]

    def add(old, new):
        return new if old is None else old + new

    acc = {}
    for m, n in PAIRS:
        c = SPEEDS[m]
        s = sum(v * v for v in c)
        gm, gn = load(m), load(n)
        groups[s] = add(groups.get(s), gm + gn)
        diff = gm - gn
        for axis in range(3):
            if c[axis]:
                key = (s, axis)
                part = diff if c[axis] > 0 else -diff
                acc[key] = part if key not in acc else (acc[key] + diff if c[axis] > 0 else acc[key] - diff)
        groups[("w", s)] = WEIGHTS[m]
        groups[("c", s)] = max(abs(v) for v in c)
    squares = sorted(k for k in groups if not isinstance(k, tuple))
    rho = WEIGHTS[0] * total
    energy = None
    for s in squares:
        part = groups[("w", s)] * groups[s]
        rho = rho + part
        energy = add(energy, float(s) * part)
        for axis in range(3):
            flux[axis] = add(flux[axis], (groups[("w", s)] * groups[("c", s)]) * acc[(s, axis)])
    cs2 = 2.0 / 3.0
    inv = 1.0 / rho
    u = [f * inv for f in flux]
    uu = u[0] * u[0] + u[1] * u[1] + u[2] * u[2]
    t = (energy * inv - uu) * (1.0 / (3.0 * cs2)) - 1.0
    b = uu * (1.0 / cs2)
    scale = rate * rho
    keep = 1.0 - rate
    w = [part * (1.0 / cs2) for part in u]
    fourth = scale * (1.0 / 24.0)
    third = scale * (1.0 / 6.0)
    bb = b * b * 0.125
    tt = t * t * 0.125
    tb = t * b * 0.25
    coeff = {}
    for s in [0] + squares:
        e = s / cs2
        k = scale * (1.0 - 0.5 * b + t * (0.5 * (e - 3.0)) + bb + tb * (5.0 - e) + tt * (e * e - 10.0 * e + 15.0))
        if s:
            l = scale * (0.5 - 0.25 * b + t * (0.25 * (e - 7.0)))
            q = scale * (1.0 - 0.5 * b + t * (0.5 * (e - 5.0)))
            coeff[s] = (k, l, q)
        else:
            coeff[s] = (k,)
    store(0, keep * total + coeff[0][0])
    for m, n in PAIRS:
        c = SPEEDS[m]
        s = sum(v * v for v in c)
        k, l, q = coeff[s]
        a = None
        for axis in range(3):
            if c[axis]:
                if a is None:
                    a = w[axis] if c[axis] > 0 else -w[axis]
                else:
                    a = a + w[axis] if c[axis] > 0 else a - w[axis]
        size = max(abs(v) for v in c)
        if size != 1:
            a = a * float(size)
        aa = a * a
        even = k + aa * (l + aa * fourth)
        odd = a * (q + aa * third)
        store(m, keep * load(m) + (even + odd))
        store(n, keep * load(n) + (even - odd))


def collide_kernel(g_ref, r_ref, w_ref, xs_ref, y_up_ref, y_down_ref, z_ref, s_ref, *, nx, ny, nz, depth):
    step = pl.program_id(0)
    lane = lax.broadcasted_iota(jnp.int32, (1, nz), 1)
    for i in range(depth):
        x = step * depth + i

        def chunk(j, i=i):
            row = j * 8

            def load(m):
                return g_ref[m, i, row : row + 8, :]

            def store(m, value):
                s_ref[m, 8 + row : 16 + row, :] = value
                if SPEEDS[m][1] != 0:
                    if j == 0:
                        s_ref[m, 8 + ny : 16 + ny, :] = value
                    if j == ny // 8 - 1:
                        s_ref[m, 0:8, :] = value

            collide_rows(load, r_ref[i, row : row + 8, :], store)

        for j in range(ny // 8):
            chunk(j)
        packed = jnp.zeros((ny, nz), F32)
        for m in list(range(Q - 1, -1, -1)):
            cx, cy, cz = SPEEDS[m]
            value = s_ref[m, 8 - cy : 8 - cy + ny, :]
            if cz:
                size = abs(cz)
                shift = (cz + ZOFF[m]) % nz if cz > 0 else ZOFF[m]
                inside = (lane >= ZOFF[m]) & (lane < ZOFF[m] + size)
                packed = jnp.where(inside, pltpu.roll(value, shift, 1) if shift else value, packed)
                value = pltpu.roll(value, cz % nz, 1)
            target = lax.rem(x + cx + nx, nx)
            w_ref[m, target] = value
            if cx:
                size = abs(cx)
                up = m if cx > 0 else OPPOSITE[m]
                slot = XOFF[up] + lax.rem(x + (size - nx % size), size)
                if cx < 0:
                    slot = jnp.where(x < size, XOFF[m] + x, slot)
                xs_ref[slot] = value
            if cy:
                ref = y_up_ref if cy > 0 else y_down_ref
                for k, row in enumerate(wrapped_rows(cy, ny)):
                    ref[YOFF[m] + k, pl.ds(x, 1), :] = value[row : row + 1, :]
        z_ref[x] = packed


def z_edge_kernel(z_low_ref, z_high_ref, y_up_ref, y_down_ref, z_out, y_up_out, y_down_out, *, nx, ny, nz):
    lane = lax.broadcasted_iota(jnp.int32, (1, 1, nz), 2)
    z_out[...] = jnp.where(lane < ZHALF, z_low_ref[...], z_high_ref[...])
    for m in range(Q):
        cx, cy, cz = SPEEDS[m]
        if not cy:
            continue
        source, out = (y_up_ref, y_up_out) if cy > 0 else (y_down_ref, y_down_out)
        for k, row in enumerate(wrapped_rows(cy, ny)):
            value = source[YOFF[m] + k]
            if cz:
                shift, mask = z_home(m, nz)
                ref = z_low_ref if cz > 0 else z_high_ref
                halo = ref[:, row, :]
                value = jnp.where(mask, pltpu.roll(halo, shift, 1) if shift else halo, value)
            out[YOFF[m] + k] = value


def y_edge_kernel(z_ref, y_low_ref, y_high_ref, out_ref, *, nx, ny, nz):
    out_ref[0:2] = z_ref[nx - 2 : nx]
    out_ref[2:4] = z_ref[0:2]
    for m, base in EOFF.items():
        cx, cy, _ = SPEEDS[m]
        size = abs(cx)
        ref = y_low_ref if cy > 0 else y_high_ref
        for k in range(abs(cy)):
            first = base + k * size
            start = nx - size if cx > 0 else 0
            out_ref[4 + first // ny, first % ny : first % ny + size, :] = ref[YOFF[m] + k, start : start + size, :]


def finish_kernel(w_ref, xr_ref, z_ref, y_low_ref, y_high_ref, edge_ref, out_ref, *, nx, ny, nz, depth):
    step = pl.program_id(0)
    for i in range(depth):
        x = step * depth + i
        for m in range(Q):
            cx, cy, cz = SPEEDS[m]
            size = abs(cx)
            source = lax.rem(x - cx + nx, nx)
            value = w_ref[m, i]
            if cx > 0:
                crossed = x < size
                layer = jnp.where(crossed, x, 0)
            elif cx < 0:
                crossed = x >= nx - size
                layer = jnp.where(crossed, x - (nx - size), 0)
            if cx:
                value = jnp.where(crossed, xr_ref[XOFF[m] + layer], value)
            if cz:
                halo = z_ref[source]
                if cx:
                    base = 2 - size if cx > 0 else 2
                    halo = jnp.where(crossed, edge_ref[base + layer], halo)
                shift, mask = z_home(m, nz)
                value = jnp.where(mask, pltpu.roll(halo, shift, 1) if shift else halo, value)
            out_ref[m, i] = value
            if cy:
                ref = y_low_ref if cy > 0 else y_high_ref
                for k, row in enumerate(wrapped_rows(cy, ny)):
                    line = ref[YOFF[m] + k, pl.ds(source, 1), :]
                    if cx:
                        first = EOFF[m] + k * size
                        other = edge_ref[4 + first // ny, pl.ds(first % ny + layer, 1), :]
                        line = jnp.where(crossed, other, line)
                    out_ref[m, i, row : row + 1, :] = line


def from_behind(block, axis, distance):
    count = lax.axis_size(axis)
    route = [((i - distance) % count, i) for i in range(count)]
    return lax.ppermute(block, axis, route)


def params(steps=0):
    if steps:
        return pltpu.CompilerParams(dimension_semantics=("arbitrary",), vmem_limit_bytes=50 * 1024 * 1024)
    return pltpu.CompilerParams(vmem_limit_bytes=50 * 1024 * 1024)


def whole(shape):
    return pl.BlockSpec(shape, lambda s: (0,) * len(shape))


def per_device(populations, relax):
    _, nx, ny, nz = populations.shape
    dims = dict(nx=nx, ny=ny, nz=nz)
    depth = 2 if nx % 2 == 0 else 1
    steps = nx // depth

    def struct(*shape):
        return jax.ShapeDtypeStruct(shape, F32)

    field = struct(Q, nx, ny, nz)
    xs = struct(2 * XHALF, ny, nz)
    ys = struct(YCOUNT, nx, nz)
    zs = struct(nx, ny, nz)
    edge = struct(4 + -(-ECOUNT // ny), ny, nz)
    cells = nx * ny * nz

    import functools

    state, x_send, y_up, y_down, z_send = pl.pallas_call(
        functools.partial(collide_kernel, depth=depth, **dims),
        grid=(steps,),
        in_specs=[
            pl.BlockSpec((Q, depth, ny, nz), lambda s: (0, s, 0, 0)),
            pl.BlockSpec((depth, ny, nz), lambda s: (s, 0, 0)),
        ],
        out_specs=[whole(a.shape) for a in (field, xs, ys, ys, zs)],
        out_shape=[field, xs, ys, ys, zs],
        scratch_shapes=[pltpu.VMEM((Q, ny + 16, nz), F32)],
        compiler_params=params(steps),
        name="collide",
    )(populations, relax)

    if lax.axis_size("gx") == 2:
        x_recv = from_behind(x_send, "gx", 1)
    else:
        x_recv = jnp.concatenate(
            [from_behind(x_send[:XHALF], "gx", 1), from_behind(x_send[XHALF:], "gx", -1)]
        )
    z_low = from_behind(z_send, "gz", 1)
    z_high = from_behind(z_send, "gz", -1)
    z_all, y_up, y_down = pl.pallas_call(
        functools.partial(z_edge_kernel, **dims),
        out_shape=[zs, ys, ys],
        compiler_params=params(),
        name="z_edge",
    )(z_low, z_high, y_up, y_down)
    y_low = from_behind(y_up, "gy", 1)
    y_high = from_behind(y_down, "gy", -1)
    edge_send = pl.pallas_call(
        functools.partial(y_edge_kernel, **dims),
        out_shape=edge,
        compiler_params=params(),
        name="y_edge",
    )(z_all, y_low, y_high)
    if lax.axis_size("gx") == 2:
        edge_recv = from_behind(edge_send, "gx", 1)
    else:
        lower = from_behind(edge_send, "gx", 1)
        upper = from_behind(edge_send, "gx", -1)
        layer = lax.broadcasted_iota(jnp.int32, edge.shape, 0)
        line = (layer - 4) * ny + lax.broadcasted_iota(jnp.int32, edge.shape, 1)
        is_low = jnp.where(layer < 4, layer < 2, line < ECOUNT // 2)
        edge_recv = jnp.where(is_low, lower, upper)
    return pl.pallas_call(
        functools.partial(finish_kernel, depth=depth, **dims),
        grid=(steps,),
        in_specs=[
            pl.BlockSpec((Q, depth, ny, nz), lambda s: (0, s, 0, 0)),
            whole(xs.shape),
            whole(zs.shape),
            whole(ys.shape),
            whole(ys.shape),
            whole(edge.shape),
        ],
        out_specs=pl.BlockSpec((Q, depth, ny, nz), lambda s: (0, s, 0, 0)),
        out_shape=field,
        compiler_params=params(steps),
        name="finish",
    )(state, x_recv, z_all, y_low, y_high, edge_recv)


def solution(mesh):
    return jax.shard_map(
        per_device,
        mesh=mesh,
        in_specs=(P(None, "gx", "gy", "gz"), P("gx", "gy", "gz")),
        out_specs=P(None, "gx", "gy", "gz"),
        check_vma=False,
    )
```

time: 100 us -> 32.1 us (0.32)
  local copies, waits for them, and re-layouts: 48.8 us -> 0.89 us
  other arithmetic: 33.1 us -> 0 us
  Pallas kernels: 0 us -> 11.5 us
  waiting for transfers between devices: 7.9 us -> 11.2 us
  between operations: 1.28 us -> 0.01 us
    unnamed x221 -> x2, local copies, waits for them, and re-layouts: 30.2 us -> 0.89 us
    another operation x20 -> x0, other arithmetic: 15 us -> none  [inbound(): return jnp.stack(layers)]
    pallas_call x0 -> x4, Pallas kernels: none -> 11.5 us  [the longest x1 6.56 us: per_device(): pl.pallas_call(functools.partial(collide_kernel, depth=depth, **dims), gr...]
    transpose x14 -> x0, other arithmetic: 11.1 us -> none  [outbound(): slabs.append(jnp.moveaxis(layers, dim - 1, 0))]
    concatenate x6 -> x0, local copies, waits for them, and re-layouts: 8.28 us -> none  [outbound(): return jnp.concatenate(slabs, axis=0)]
    transpose x12 -> x0, local copies, waits for them, and re-layouts: 8.19 us -> none  [the longest x6 5.21 us: inbound(): slab = jnp.moveaxis(from_upper[upper_offset:upper_offset - speed], 0, axis)]
    sub x4 -> x0, other arithmetic: 7.04 us -> none  [collide(): results.append(popul[member] - rate * (popul[member] - maxwellian_target))]
    ppermute x6, waiting for transfers between devices: 7.9 us -> 11.2 us  [from_behind(): return lax.ppermute(block, axis, route)]
  transfers between devices with their start and end apart: 6 -> 6, of which waited for: 3 -> 4; matrix products, arithmetic and copies ran while one was open for 25% -> 0% of each run, Pallas kernels for 0% -> 0%
where the time goes in v1:
time: 32.1 us; the launch traced here: 31.8 us
  Pallas kernels  11.5 us (36%)
  waiting for transfers between devices  11.2 us (35%)
  starting transfers between devices  8.12 us (25%)
  local copies, waits for them, and re-layouts  0.89 us (3%)
    ppermute x6, waiting for transfers between devices, from_behind(): return lax.ppermute(block, axis, route)  11.2 us
    ppermute x6, starting transfers between devices, from_behind(): return lax.ppermute(block, axis, route)  8.12 us
    pallas_call x1, Pallas kernels, per_device(): pl.pallas_call(functools.partial(collide_kernel, depth=depth, **dims), gr...  6.56 us
    pallas_call x1, Pallas kernels, per_device(): pl.pallas_call(functools.partial(finish_kernel, depth=depth, **dims), gri...  4.85 us
    unnamed x2, local copies, waits for them, and re-layouts  0.89 us
  transfers between devices with their start and end apart: 6, of which 4 were waited for; matrix products, arithmetic and copies ran while one was open for 0% of the time, Pallas kernels for 0%

profile of v1, /device:TPU:0, one launch (start us, length us, event | category | flops | bytes accessed | tf_op | source)
XLA Modules:
  0.0 31.8 jit_solution(13237167507591478276)
XLA Ops:
  0.0 0.0 copy-start
  0.0 0.9 %copy-done = f32[8,24,128]{2,1,0:T(8,128)S(1)} copy-done((f32[8,24,128]{2,1,0:T(8,128)S(1)}, f32[8,24,128]{2,1,0:T(8,128)}, u32[]{:S(2)}) %copy-start) | copy-done | bytes 98328
  0.9 6.6 %collide.1 = (f32[39,8,24,128]{3,2,1,0:T(8,128)}, f32[36,24,128]{2,1,0:T(8,128)S(1)}, f32[18,8,128]{2,1,0:T(8,128)S(1)}, f32[18,8,128]{2,1,0:T(8,128)S(1)}, f32[8,24,128]{2,1,0:T(8,128)S(1)}) custom-call(f32[39,8,24,128]{3,2,1,0:T(8,128)} %g_ref.1, f32[8,24,128]{2,1,0:T(8,128)S(1)} %copy-done), custom_call_target="tpu_custom_call" | custom-call | tf_op jit(solution)/shard_map/collide/pallas_call | solution.py:327
  7.5 3.0 %collective-permute-start = (f32[36,24,128]{2,1,0:T(8,128)S(1)}, f32[36,24,128]{2,1,0:T(8,128)S(1)}, u32[]{:S(2)}, u32[]{:S(2)}) collective-permute-start(f32[36,24,128]{2,1,0:T(8,128)S(1)} %get-tuple-element.14), channel_id=1, source_target_pairs={{16,0},{0,16},{17,1},{1,17},{18,2},{2,18},{19,3},{3,19},{20,4},{4,... | collective-permute-start | bytes 1327112 | tf_op jit(solution)/shard_map/ppermute | solution.py:296
  10.4 0.7 %collective-permute-start.2 = (f32[8,24,128]{2,1,0:T(8,128)S(1)}, f32[8,24,128]{2,1,0:T(8,128)S(1)}, u32[]{:S(2)}, u32[]{:S(2)}) collective-permute-start(f32[8,24,128]{2,1,0:T(8,128)S(1)} %get-tuple-element.15), channel_id=1, source_target_pairs={{1,0},{2,1},{3,2},{0,3},{5,4},{6,5},{7,6},{4,7},{9,8},{10,9},{11,1... | collective-permute-start | bytes 294920 | tf_op jit(solution)/shard_map/ppermute | solution.py:296
  11.1 0.0 collective-permute-start.1
  11.1 2.9 %collective-permute-done.2.z_high_ref = f32[8,24,128]{2,1,0:T(8,128)S(1)} collective-permute-done((f32[8,24,128]{2,1,0:T(8,128)S(1)}, f32[8,24,128]{2,1,0:T(8,128)S(1)}, u32[]{:S(2)}, u32[]{:S(2)}) %collective-permute-start.2) | collective-permute-done | bytes 98336 | tf_op jit(solution)/shard_map/ppermute | solution.py:296
  14.0 1.6 %collective-permute-done.1.z_low_ref = f32[8,24,128]{2,1,0:T(8,128)S(1)} collective-permute-done((f32[8,24,128]{2,1,0:T(8,128)S(1)}, f32[8,24,128]{2,1,0:T(8,128)S(1)}, u32[]{:S(2)}, u32[]{:S(2)}) %collective-permute-start.1) | collective-permute-done | bytes 98336 | tf_op jit(solution)/shard_map/ppermute | solution.py:296
  15.6 0.1 z_edge.1
  15.7 1.6 %collective-permute-start.3 = (f32[18,8,128]{2,1,0:T(8,128)S(1)}, f32[18,8,128]{2,1,0:T(8,128)S(1)}, u32[]{:S(2)}, u32[]{:S(2)}) collective-permute-start(f32[18,8,128]{2,1,0:T(8,128)S(1)} %get-tuple-element.19), channel_id=1, source_target_pairs={{12,0},{0,4},{4,8},{8,12},{13,1},{1,5},{5,9},{9,13},{14,2},{2,6},{... | collective-permute-start | bytes 221192 | tf_op jit(solution)/shard_map/ppermute | solution.py:296
  17.3 2.2 %collective-permute-start.4 = (f32[18,8,128]{2,1,0:T(8,128)S(1)}, f32[18,8,128]{2,1,0:T(8,128)S(1)}, u32[]{:S(2)}, u32[]{:S(2)}) collective-permute-start(f32[18,8,128]{2,1,0:T(8,128)S(1)} %get-tuple-element.20), channel_id=1, source_target_pairs={{4,0},{8,4},{12,8},{0,12},{5,1},{9,5},{13,9},{1,13},{6,2},{10,6},{... | collective-permute-start | bytes 221192 | tf_op jit(solution)/shard_map/ppermute | solution.py:296
  19.6 3.1 %collective-permute-done.3.y_low_ref = f32[18,8,128]{2,1,0:T(8,128)S(1)} collective-permute-done((f32[18,8,128]{2,1,0:T(8,128)S(1)}, f32[18,8,128]{2,1,0:T(8,128)S(1)}, u32[]{:S(2)}, u32[]{:S(2)}) %collective-permute-start.3) | collective-permute-done | bytes 73760 | tf_op jit(solution)/shard_map/ppermute | solution.py:296
  22.6 0.0 collective-permute-done.4.y_high_ref
  22.6 0.6 %collective-permute-start.5 = (f32[5,24,128]{2,1,0:T(8,128)S(1)}, f32[5,24,128]{2,1,0:T(8,128)S(1)}, u32[]{:S(2)}, u32[]{:S(2)}) collective-permute-start(f32[5,24,128]{2,1,0:T(8,128)S(1)} %y_edge.1), channel_id=1, source_target_pairs={{16,0},{0,16},{17,1},{1,17},{18,2},{2,18},{19,3},{3,19},{20,4},{4,... | collective-permute-start | bytes 184328 | tf_op jit(solution)/shard_map/ppermute | solution.py:296
  23.2 3.7 %collective-permute-done.5.edge_ref = f32[5,24,128]{2,1,0:T(8,128)S(1)} collective-permute-done((f32[5,24,128]{2,1,0:T(8,128)S(1)}, f32[5,24,128]{2,1,0:T(8,128)S(1)}, u32[]{:S(2)}, u32[]{:S(2)}) %collective-permute-start.5) | collective-permute-done | bytes 61472 | tf_op jit(solution)/shard_map/ppermute | solution.py:296
  26.9 0.0 collective-permute-done.xr_ref
  26.9 4.9 %finish.1 = f32[39,8,24,128]{3,2,1,0:T(8,128)} custom-call(f32[39,8,24,128]{3,2,1,0:T(8,128)} %get-tuple-element.13.w_ref, f32[36,24,128]{2,1,0:T(8,128)S(1)} %collective-permute-done.xr_ref, f32[8,24,128]{2,1,0:T(8,128)S(1)} %get-tuple-element.18.z_ref, f32[18,8,128]{2,1,0:T(8,128)S(1)} %collective-permute-done.3.y_low_ref, ...), custom_call_target="tpu_custom_call" | custom-call | tf_op jit(solution)/shard_map/finish/pallas_call | solution.py:372
  (1 shorter events, 0.0 us)
Async XLA Ops:
  0.0 0.9 %copy-start = (f32[8,24,128]{2,1,0:T(8,128)S(1)}, f32[8,24,128]{2,1,0:T(8,128)}, u32[]{:S(2)}) copy-start(f32[8,24,128]{2,1,0:T(8,128)} %r_ref.1) | copy-start | bytes 294916
  7.5 19.5 %collective-permute-start = (f32[36,24,128]{2,1,0:T(8,128)S(1)}, f32[36,24,128]{2,1,0:T(8,128)S(1)}, u32[]{:S(2)}, u32[]{:S(2)}) collective-permute-start(f32[36,24,128]{2,1,0:T(8,128)S(1)} %get-tuple-element.14), channel_id=1, source_target_pairs={{16,0},{0,16},{17,1},{1,17},{18,2},{2,18},{19,3},{3,19},{20,4},{4,... | collective-permute-start | bytes 1327112 | tf_op jit(solution)/shard_map/ppermute | solution.py:296
  10.4 3.6 %collective-permute-start.2 = (f32[8,24,128]{2,1,0:T(8,128)S(1)}, f32[8,24,128]{2,1,0:T(8,128)S(1)}, u32[]{:S(2)}, u32[]{:S(2)}) collective-permute-start(f32[8,24,128]{2,1,0:T(8,128)S(1)} %get-tuple-element.15), channel_id=1, source_target_pairs={{1,0},{2,1},{3,2},{0,3},{5,4},{6,5},{7,6},{4,7},{9,8},{10,9},{11,1... | collective-permute-start | bytes 294920 | tf_op jit(solution)/shard_map/ppermute | solution.py:296
  11.1 4.5 %collective-permute-start.1 = (f32[8,24,128]{2,1,0:T(8,128)S(1)}, f32[8,24,128]{2,1,0:T(8,128)S(1)}, u32[]{:S(2)}, u32[]{:S(2)}) collective-permute-start(f32[8,24,128]{2,1,0:T(8,128)S(1)} %get-tuple-element.15), channel_id=1, source_target_pairs={{3,0},{0,1},{1,2},{2,3},{7,4},{4,5},{5,6},{6,7},{11,8},{8,9},{9,10... | collective-permute-start | bytes 294920 | tf_op jit(solution)/shard_map/ppermute | solution.py:296
  15.7 6.9 %collective-permute-start.3 = (f32[18,8,128]{2,1,0:T(8,128)S(1)}, f32[18,8,128]{2,1,0:T(8,128)S(1)}, u32[]{:S(2)}, u32[]{:S(2)}) collective-permute-start(f32[18,8,128]{2,1,0:T(8,128)S(1)} %get-tuple-element.19), channel_id=1, source_target_pairs={{12,0},{0,4},{4,8},{8,12},{13,1},{1,5},{5,9},{9,13},{14,2},{2,6},{... | collective-permute-start | bytes 221192 | tf_op jit(solution)/shard_map/ppermute | solution.py:296
  17.3 5.3 %collective-permute-start.4 = (f32[18,8,128]{2,1,0:T(8,128)S(1)}, f32[18,8,128]{2,1,0:T(8,128)S(1)}, u32[]{:S(2)}, u32[]{:S(2)}) collective-permute-start(f32[18,8,128]{2,1,0:T(8,128)S(1)} %get-tuple-element.20), channel_id=1, source_target_pairs={{4,0},{8,4},{12,8},{0,12},{5,1},{9,5},{13,9},{1,13},{6,2},{10,6},{... | collective-permute-start | bytes 221192 | tf_op jit(solution)/shard_map/ppermute | solution.py:296
  22.6 4.3 %collective-permute-start.5 = (f32[5,24,128]{2,1,0:T(8,128)S(1)}, f32[5,24,128]{2,1,0:T(8,128)S(1)}, u32[]{:S(2)}, u32[]{:S(2)}) collective-permute-start(f32[5,24,128]{2,1,0:T(8,128)S(1)} %y_edge.1), channel_id=1, source_target_pairs={{16,0},{0,16},{17,1},{1,17},{18,2},{2,18},{19,3},{3,19},{20,4},{4,... | collective-permute-start | bytes 184328 | tf_op jit(solution)/shard_map/ppermute | solution.py:296

commit v2 on v1

--- a/solution.py
+++ b/solution.py
@@ -1,3 +1,5 @@
+import functools
+
 import jax
 import jax.numpy as jnp
 from jax import lax
@@ -254,40 +256,54 @@
             out_ref[4 + first // ny, first % ny : first % ny + size, :] = ref[YOFF[m] + k, start : start + size, :]
 
 
-def finish_kernel(w_ref, xr_ref, z_ref, y_low_ref, y_high_ref, edge_ref, out_ref, *, nx, ny, nz, depth):
+def inner_kernel(w_ref, z_ref, y_low_ref, y_high_ref, out_ref, *, nx, ny, nz, depth):
     step = pl.program_id(0)
     for i in range(depth):
         x = step * depth + i
         for m in range(Q):
             cx, cy, cz = SPEEDS[m]
-            size = abs(cx)
             source = lax.rem(x - cx + nx, nx)
             value = w_ref[m, i]
-            if cx > 0:
-                crossed = x < size
-                layer = jnp.where(crossed, x, 0)
-            elif cx < 0:
-                crossed = x >= nx - size
-                layer = jnp.where(crossed, x - (nx - size), 0)
-            if cx:
-                value = jnp.where(crossed, xr_ref[XOFF[m] + layer], value)
             if cz:
                 halo = z_ref[source]
-                if cx:
-                    base = 2 - size if cx > 0 else 2
-                    halo = jnp.where(crossed, edge_ref[base + layer], halo)
                 shift, mask = z_home(m, nz)
                 value = jnp.where(mask, pltpu.roll(halo, shift, 1) if shift else halo, value)
             out_ref[m, i] = value
             if cy:
                 ref = y_low_ref if cy > 0 else y_high_ref
                 for k, row in enumerate(wrapped_rows(cy, ny)):
-                    line = ref[YOFF[m] + k, pl.ds(source, 1), :]
-                    if cx:
-                        first = EOFF[m] + k * size
-                        other = edge_ref[4 + first // ny, pl.ds(first % ny + layer, 1), :]
-                        line = jnp.where(crossed, other, line)
-                    out_ref[m, i, row : row + 1, :] = line
+                    out_ref[m, i, row : row + 1, :] = ref[YOFF[m] + k, pl.ds(source, 1), :]
+
+
+def outer_kernel(inner_ref, xr_ref, edge_ref, out_ref, layers_ref, sems, *, nx, ny, nz):
+    copies = []
+    for m, slot in XOFF.items():
+        cx, cy, cz = SPEEDS[m]
+        size = abs(cx)
+        plain = cy == 0 and cz == 0
+        if not plain:
+            for layer in range(size):
+                value = xr_ref[slot + layer]
+                if cz:
+                    halo = edge_ref[(2 - size if cx > 0 else 2) + layer]
+                    shift, mask = z_home(m, nz)
+                    value = jnp.where(mask, pltpu.roll(halo, shift, 1) if shift else halo, value)
+                layers_ref[slot + layer] = value
+                if cy:
+                    for k, row in enumerate(wrapped_rows(cy, ny)):
+                        line = EOFF[m] + k * size + layer
+                        at = (4 + line // ny, slice(line % ny, line % ny + 1))
+                        layers_ref[slot + layer, row : row + 1, :] = edge_ref[at[0], at[1], :]
+        start = 0 if cx > 0 else nx - size
+        copy = pltpu.make_async_copy(
+            (xr_ref if plain else layers_ref).at[pl.ds(slot, size)],
+            out_ref.at[m, pl.ds(start, size)],
+            sems.at[len(copies)],
+        )
+        copy.start()
+        copies.append(copy)
+    for copy in copies:
+        copy.wait()
 
 
 def from_behind(block, axis, distance):
@@ -321,8 +337,6 @@
     zs = struct(nx, ny, nz)
     edge = struct(4 + -(-ECOUNT // ny), ny, nz)
     cells = nx * ny * nz
-
-    import functools
 
     state, x_send, y_up, y_down, z_send = pl.pallas_call(
         functools.partial(collide_kernel, depth=depth, **dims),
@@ -369,22 +383,35 @@
         line = (layer - 4) * ny + lax.broadcasted_iota(jnp.int32, edge.shape, 1)
         is_low = jnp.where(layer < 4, layer < 2, line < ECOUNT // 2)
         edge_recv = jnp.where(is_low, lower, upper)
-    return pl.pallas_call(
-        functools.partial(finish_kernel, depth=depth, **dims),
+    inner = pl.pallas_call(
+        functools.partial(inner_kernel, depth=depth, **dims),
         grid=(steps,),
         in_specs=[
             pl.BlockSpec((Q, depth, ny, nz), lambda s: (0, s, 0, 0)),
-            whole(xs.shape),
             whole(zs.shape),
             whole(ys.shape),
             whole(ys.shape),
-            whole(edge.shape),
         ],
         out_specs=pl.BlockSpec((Q, depth, ny, nz), lambda s: (0, s, 0, 0)),
         out_shape=field,
         compiler_params=params(steps),
-        name="finish",
-    )(state, x_recv, z_all, y_low, y_high, edge_recv)
+        cost_estimate=pl.CostEstimate(flops=400 * cells, bytes_accessed=8 * Q * cells, transcendentals=0),
+        name="inner",
+    )(state, z_all, y_low, y_high)
+    return pl.pallas_call(
+        functools.partial(outer_kernel, **dims),
+        in_specs=[
+            pl.BlockSpec(memory_space=pl.ANY),
+            pl.BlockSpec(memory_space=pltpu.VMEM),
+            pl.BlockSpec(memory_space=pltpu.VMEM),
+        ],
+        out_specs=pl.BlockSpec(memory_space=pl.ANY),
+        out_shape=field,
+        input_output_aliases={0: 0},
+        scratch_shapes=[pltpu.VMEM(xs.shape, F32), pltpu.SemaphoreType.DMA((len(XOFF),))],
+        compiler_params=params(),
+        name="outer",
+    )(inner, x_recv, edge_recv)
 
 
 def solution(mesh):

time: 32.1 us -> 29.4 us (0.916)
  waiting for transfers between devices: 11.2 us -> 7.54 us
  local copies, waits for them, and re-layouts: 0.89 us -> 2.98 us
  Pallas kernels: 11.5 us -> 10.5 us
    ppermute x6, waiting for transfers between devices: 11.2 us -> 7.54 us  [from_behind(): return lax.ppermute(block, axis, route)]
    unnamed x2 -> x4, local copies, waits for them, and re-layouts: 0.89 us -> 2.98 us
    pallas_call x1 -> x2, Pallas kernels: 4.85 us -> 3.82 us  [the longest x1 2.81 us: per_device(): pl.pallas_call(functools.partial(inner_kernel, depth=depth, **dims), grid...]
  transfers between devices with their start and end apart: 6 -> 6, of which waited for: 4 -> 3; matrix products, arithmetic and copies ran while one was open for 0% -> 0% of each run, Pallas kernels for 0% -> 10%
where the time goes in v2:
time: 29.4 us; the launch traced here: 29.2 us
  Pallas kernels  10.5 us (36%)
  starting transfers between devices  8.12 us (28%)
  waiting for transfers between devices  7.54 us (26%)
  local copies, waits for them, and re-layouts  2.98 us (10%)
    ppermute x6, starting transfers between devices, from_behind(): return lax.ppermute(block, axis, route)  8.12 us
    ppermute x6, waiting for transfers between devices, from_behind(): return lax.ppermute(block, axis, route)  7.54 us
    pallas_call x1, Pallas kernels, per_device(): pl.pallas_call(functools.partial(collide_kernel, depth=depth, **dims), gr...  6.62 us
    unnamed x4, local copies, waits for them, and re-layouts  2.98 us
    pallas_call x1, Pallas kernels, per_device(): pl.pallas_call(functools.partial(inner_kernel, depth=depth, **dims), grid...  2.81 us
    pallas_call x1, Pallas kernels, per_device(): pl.pallas_call(functools.partial(outer_kernel, **dims), in_specs=[pl.Bloc...  1.01 us
  transfers between devices with their start and end apart: 6, of which 3 were waited for; matrix products, arithmetic and copies ran while one was open for 0% of the time, Pallas kernels for 10%

profile of v2, /device:TPU:0, one launch (start us, length us, event | category | flops | bytes accessed | tf_op | source)
XLA Modules:
  0.0 29.2 jit_solution(17907584056304219440)
XLA Ops:
  0.0 0.0 copy-start.1
  0.0 0.9 %copy-done.1 = f32[8,24,128]{2,1,0:T(8,128)S(1)} copy-done((f32[8,24,128]{2,1,0:T(8,128)S(1)}, f32[8,24,128]{2,1,0:T(8,128)}, u32[]{:S(2)}) %copy-start.1) | copy-done | bytes 98328
  0.9 6.6 %collide.1 = (f32[39,8,24,128]{3,2,1,0:T(8,128)}, f32[36,24,128]{2,1,0:T(8,128)S(1)}, f32[18,8,128]{2,1,0:T(8,128)S(1)}, f32[18,8,128]{2,1,0:T(8,128)S(1)}, f32[8,24,128]{2,1,0:T(8,128)S(1)}) custom-call(f32[39,8,24,128]{3,2,1,0:T(8,128)} %g_ref.1, f32[8,24,128]{2,1,0:T(8,128)S(1)} %copy-done.1), custom_call_target="tpu_custom_call" | custom-call | tf_op jit(solution)/shard_map/collide/pallas_call | solution.py:341
  7.5 3.0 %collective-permute-start.4 = (f32[36,24,128]{2,1,0:T(8,128)S(1)}, f32[36,24,128]{2,1,0:T(8,128)S(1)}, u32[]{:S(2)}, u32[]{:S(2)}) collective-permute-start(f32[36,24,128]{2,1,0:T(8,128)S(1)} %get-tuple-element.20), channel_id=1, source_target_pairs={{16,0},{0,16},{17,1},{1,17},{18,2},{2,18},{19,3},{3,19},{20,4},{4,... | collective-permute-start | bytes 1327112 | tf_op jit(solution)/shard_map/ppermute | solution.py:312
  10.5 0.7 %collective-permute-start.1 = (f32[8,24,128]{2,1,0:T(8,128)S(1)}, f32[8,24,128]{2,1,0:T(8,128)S(1)}, u32[]{:S(2)}, u32[]{:S(2)}) collective-permute-start(f32[8,24,128]{2,1,0:T(8,128)S(1)} %get-tuple-element.14), channel_id=1, source_target_pairs={{1,0},{2,1},{3,2},{0,3},{5,4},{6,5},{7,6},{4,7},{9,8},{10,9},{11,1... | collective-permute-start | bytes 294920 | tf_op jit(solution)/shard_map/ppermute | solution.py:312
  11.2 0.0 collective-permute-start
  11.2 2.9 %collective-permute-done.1.z_high_ref = f32[8,24,128]{2,1,0:T(8,128)S(1)} collective-permute-done((f32[8,24,128]{2,1,0:T(8,128)S(1)}, f32[8,24,128]{2,1,0:T(8,128)S(1)}, u32[]{:S(2)}, u32[]{:S(2)}) %collective-permute-start.1) | collective-permute-done | bytes 98336 | tf_op jit(solution)/shard_map/ppermute | solution.py:312
  14.1 1.6 %collective-permute-done.z_low_ref = f32[8,24,128]{2,1,0:T(8,128)S(1)} collective-permute-done((f32[8,24,128]{2,1,0:T(8,128)S(1)}, f32[8,24,128]{2,1,0:T(8,128)S(1)}, u32[]{:S(2)}, u32[]{:S(2)}) %collective-permute-start) | collective-permute-done | bytes 98336 | tf_op jit(solution)/shard_map/ppermute | solution.py:312
  15.6 0.1 z_edge.1
  15.7 1.6 %collective-permute-start.2 = (f32[18,8,128]{2,1,0:T(8,128)S(1)}, f32[18,8,128]{2,1,0:T(8,128)S(1)}, u32[]{:S(2)}, u32[]{:S(2)}) collective-permute-start(f32[18,8,128]{2,1,0:T(8,128)S(1)} %get-tuple-element.18), channel_id=1, source_target_pairs={{12,0},{0,4},{4,8},{8,12},{13,1},{1,5},{5,9},{9,13},{14,2},{2,6},{... | collective-permute-start | bytes 221192 | tf_op jit(solution)/shard_map/ppermute | solution.py:312
  17.4 2.2 %collective-permute-start.3 = (f32[18,8,128]{2,1,0:T(8,128)S(1)}, f32[18,8,128]{2,1,0:T(8,128)S(1)}, u32[]{:S(2)}, u32[]{:S(2)}) collective-permute-start(f32[18,8,128]{2,1,0:T(8,128)S(1)} %get-tuple-element.19), channel_id=1, source_target_pairs={{4,0},{8,4},{12,8},{0,12},{5,1},{9,5},{13,9},{1,13},{6,2},{10,6},{... | collective-permute-start | bytes 221192 | tf_op jit(solution)/shard_map/ppermute | solution.py:312
  19.6 3.1 %collective-permute-done.2.y_low_ref = f32[18,8,128]{2,1,0:T(8,128)S(1)} collective-permute-done((f32[18,8,128]{2,1,0:T(8,128)S(1)}, f32[18,8,128]{2,1,0:T(8,128)S(1)}, u32[]{:S(2)}, u32[]{:S(2)}) %collective-permute-start.2) | collective-permute-done | bytes 73760 | tf_op jit(solution)/shard_map/ppermute | solution.py:312
  22.7 0.0 collective-permute-done.3.y_high_ref
  22.7 0.6 %collective-permute-start.5 = (f32[5,24,128]{2,1,0:T(8,128)S(1)}, f32[5,24,128]{2,1,0:T(8,128)S(1)}, u32[]{:S(2)}, u32[]{:S(2)}) collective-permute-start(f32[5,24,128]{2,1,0:T(8,128)S(1)} %y_edge.1), channel_id=1, source_target_pairs={{16,0},{0,16},{17,1},{1,17},{18,2},{2,18},{19,3},{3,19},{20,4},{4,... | collective-permute-start | bytes 184328 | tf_op jit(solution)/shard_map/ppermute | solution.py:312
  23.3 0.0 copy-start
  23.3 2.1 %copy-done = f32[39,8,24,128]{3,2,1,0:T(8,128)S(1)} copy-done((f32[39,8,24,128]{3,2,1,0:T(8,128)S(1)}, f32[39,8,24,128]{3,2,1,0:T(8,128)}, u32[]{:S(2)}) %copy-start) | copy-done | bytes 3833880
  25.4 2.8 %inner.1.inner_ref = f32[39,8,24,128]{3,2,1,0:T(8,128)} custom-call(f32[39,8,24,128]{3,2,1,0:T(8,128)S(1)} %copy-done, f32[8,24,128]{2,1,0:T(8,128)S(1)} %get-tuple-element.17.z_ref, f32[18,8,128]{2,1,0:T(8,128)S(1)} %collective-permute-done.2.y_low_ref, f32[18,8,128]{2,1,0:T(8,128)S(1)} %collective-permute-done.3.y_high_ref), custom_call_target="tpu_custom_call" | custom-call | flops 9830400 | bytes 7667712 | tf_op jit(solution)/shard_map/inner/pallas_call | solution.py:386
  28.2 0.0 collective-permute-done.5.edge_ref
  28.2 0.0 collective-permute-done.4.xr_ref
  28.2 1.0 %outer.1 = f32[39,8,24,128]{3,2,1,0:T(8,128)} custom-call(f32[39,8,24,128]{3,2,1,0:T(8,128)} %inner.1.inner_ref, f32[36,24,128]{2,1,0:T(8,128)S(1)} %collective-permute-done.4.xr_ref, f32[5,24,128]{2,1,0:T(8,128)S(1)} %collective-permute-done.5.edge_ref), custom_call_target="tpu_custom_call", output_to_operand_aliasing={{}: (0, {})} | custom-call | tf_op jit(solution)/shard_map/outer/pallas_call | solution.py:401
  (1 shorter events, 0.0 us)
Async XLA Ops:
  0.0 0.9 %copy-start.1 = (f32[8,24,128]{2,1,0:T(8,128)S(1)}, f32[8,24,128]{2,1,0:T(8,128)}, u32[]{:S(2)}) copy-start(f32[8,24,128]{2,1,0:T(8,128)} %r_ref.1) | copy-start | bytes 294916
  7.5 20.7 %collective-permute-start.4 = (f32[36,24,128]{2,1,0:T(8,128)S(1)}, f32[36,24,128]{2,1,0:T(8,128)S(1)}, u32[]{:S(2)}, u32[]{:S(2)}) collective-permute-start(f32[36,24,128]{2,1,0:T(8,128)S(1)} %get-tuple-element.20), channel_id=1, source_target_pairs={{16,0},{0,16},{17,1},{1,17},{18,2},{2,18},{19,3},{3,19},{20,4},{4,... | collective-permute-start | bytes 1327112 | tf_op jit(solution)/shard_map/ppermute | solution.py:312
  10.5 3.6 %collective-permute-start.1 = (f32[8,24,128]{2,1,0:T(8,128)S(1)}, f32[8,24,128]{2,1,0:T(8,128)S(1)}, u32[]{:S(2)}, u32[]{:S(2)}) collective-permute-start(f32[8,24,128]{2,1,0:T(8,128)S(1)} %get-tuple-element.14), channel_id=1, source_target_pairs={{1,0},{2,1},{3,2},{0,3},{5,4},{6,5},{7,6},{4,7},{9,8},{10,9},{11,1... | collective-permute-start | bytes 294920 | tf_op jit(solution)/shard_map/ppermute | solution.py:312
  11.2 4.5 %collective-permute-start = (f32[8,24,128]{2,1,0:T(8,128)S(1)}, f32[8,24,128]{2,1,0:T(8,128)S(1)}, u32[]{:S(2)}, u32[]{:S(2)}) collective-permute-start(f32[8,24,128]{2,1,0:T(8,128)S(1)} %get-tuple-element.14), channel_id=1, source_target_pairs={{3,0},{0,1},{1,2},{2,3},{7,4},{4,5},{5,6},{6,7},{11,8},{8,9},{9,10... | collective-permute-start | bytes 294920 | tf_op jit(solution)/shard_map/ppermute | solution.py:312
  15.7 6.9 %collective-permute-start.2 = (f32[18,8,128]{2,1,0:T(8,128)S(1)}, f32[18,8,128]{2,1,0:T(8,128)S(1)}, u32[]{:S(2)}, u32[]{:S(2)}) collective-permute-start(f32[18,8,128]{2,1,0:T(8,128)S(1)} %get-tuple-element.18), channel_id=1, source_target_pairs={{12,0},{0,4},{4,8},{8,12},{13,1},{1,5},{5,9},{9,13},{14,2},{2,6},{... | collective-permute-start | bytes 221192 | tf_op jit(solution)/shard_map/ppermute | solution.py:312
  17.4 5.3 %collective-permute-start.3 = (f32[18,8,128]{2,1,0:T(8,128)S(1)}, f32[18,8,128]{2,1,0:T(8,128)S(1)}, u32[]{:S(2)}, u32[]{:S(2)}) collective-permute-start(f32[18,8,128]{2,1,0:T(8,128)S(1)} %get-tuple-element.19), channel_id=1, source_target_pairs={{4,0},{8,4},{12,8},{0,12},{5,1},{9,5},{13,9},{1,13},{6,2},{10,6},{... | collective-permute-start | bytes 221192 | tf_op jit(solution)/shard_map/ppermute | solution.py:312
  22.7 5.5 %collective-permute-start.5 = (f32[5,24,128]{2,1,0:T(8,128)S(1)}, f32[5,24,128]{2,1,0:T(8,128)S(1)}, u32[]{:S(2)}, u32[]{:S(2)}) collective-permute-start(f32[5,24,128]{2,1,0:T(8,128)S(1)} %y_edge.1), channel_id=1, source_target_pairs={{16,0},{0,16},{17,1},{1,17},{18,2},{2,18},{19,3},{3,19},{20,4},{4,... | collective-permute-start | bytes 184328 | tf_op jit(solution)/shard_map/ppermute | solution.py:312
  23.3 2.1 %copy-start = (f32[39,8,24,128]{3,2,1,0:T(8,128)S(1)}, f32[39,8,24,128]{3,2,1,0:T(8,128)}, u32[]{:S(2)}) copy-start(f32[39,8,24,128]{3,2,1,0:T(8,128)} %get-tuple-element.13.w_ref) | copy-start | bytes 11501572
